TPU v7x, 32 devices: a whole 2x2x4 slice. The times are simulated.
32 devices in a mesh: task: 8 (over z, core), tp: 4 (over y, x).
Axes of the slice: x: 2, y: 2, z: 4, core: 2. Of those that a mesh axis runs over, the one named last changes fastest.
Arguments:
- support_x: bfloat16 [8, 384, 3584], P('task'), may hold values from -6 to 6
- adapter_a: bfloat16 [8, 3584, 64], P('task'), may hold values from -0.09375 to 0.09375
- gate_pre: bfloat16 [8, 384, 10240], P('task', None, 'tp'), may hold values from -6 to 6
- lengths: int32 [8], P('task'), may hold values from 128 to 384, as said below
- damping: float32 [8], P('task'), may hold values from 0.03 to 0.3
- down_w: bfloat16 [10240, 3584], P('tp', 'task'), may hold values from -0.0625 to 0.0625
- grad_b: float32 [8, 64, 10240], P('task', None, 'tp'), may hold values from -6 to 6
Outputs:
- solution: float32 [8, 64, 10240], P('task', None, 'tp')
- residual: float32 [8, 64, 10240], P('task', None, 'tp')
Inputs may be any that keep to these rules, and one draw needn't show every extreme that they name: `lengths`: each a multiple of 128; some task has exactly 384.
All inputs are finite; a program needn't handle non-finite values.
Results may differ from a plain program's by a relative error of at most 0.033.
Values may be sent and summed in bfloat16 or wider, within the bound.
A program may use at most 64 MiB of HBM per device.

v0:
```python
import jax
import jax.numpy as jnp
from jax import lax
from jax.sharding import PartitionSpec as P

ITERS = 2


def shards(support_x, adapter_a, gate_pre, lengths, damping, down_w, grad_b):
    down_full = lax.all_gather(down_w, "task", axis=1, tiled=True)
    features = jnp.dot(support_x[0], adapter_a[0], preferred_element_type=jnp.float32).astype(
        jnp.bfloat16
    )
    positions = lax.broadcasted_iota(jnp.int32, (gate_pre.shape[1], 1), 0)
    gated = jnp.where(
        positions < lengths[0], jax.nn.silu(gate_pre[0].astype(jnp.float32)), 0.0
    ).astype(jnp.bfloat16)
    tokens_live = lengths[0].astype(jnp.float32)
    damping_rate = damping[0]

    def transposed(mixed_rows):
        return lax.dot_general(
            mixed_rows, down_full, (((1,), (1,)), ((), ())), preferred_element_type=jnp.float32
        )

    def apply(vector):
        inner = jnp.dot(features, vector.astype(jnp.bfloat16), preferred_element_type=jnp.float32)
        active = (gated * inner).astype(jnp.bfloat16)
        partial_sum = jnp.dot(active, down_full, preferred_element_type=jnp.float32)
        mixed = lax.psum(partial_sum.astype(jnp.bfloat16), "tp")
        second = (gated * transposed(mixed)).astype(jnp.bfloat16)
        product = lax.dot_general(
            features, second, (((0,), (0,)), ((), ())), preferred_element_type=jnp.float32
        )
        return product / tokens_live + damping_rate * vector

    def paired_sums(vector, image):
        return lax.psum((jnp.sum(vector * vector), jnp.sum(vector * image)), "tp")

    target = grad_b[0]
    solution = jnp.zeros_like(target)
    residual = target
    image = apply(residual)
    norm_now, product = paired_sums(residual, image)
    alpha = norm_now / product
    direction, along = (residual, image)
    for step in range(ITERS):
        solution = solution + alpha * direction
        residual = residual - alpha * along
        if step + 1 < ITERS:
            image = apply(residual)
            norm_next, product = paired_sums(residual, image)
            ratio = norm_next / norm_now
            alpha = norm_next / (product - ratio * norm_next / alpha)
            direction = residual + ratio * direction
            along = image + ratio * along
            norm_now = norm_next
    return (solution[None], residual[None])


def solution(mesh):
    in_specs = (
        P("task", None, None),
        P("task", None, None),
        P("task", None, "tp"),
        P("task"),
        P("task"),
        P("tp", "task"),
        P("task", None, "tp"),
    )
    out_specs = (P("task", None, "tp"), P("task", None, "tp"))
    return jax.shard_map(shards, mesh=mesh, in_specs=in_specs, out_specs=out_specs, check_vma=False)
```

profile of v0, /device:TPU:0, one launch (start us, length us, event | category | flops | bytes accessed | tf_op | source)
XLA Modules:
  0.0 429.8 jit_solution(7831728093009791851)
XLA Ops:
  7.2 0.0 copy-start
  7.2 0.0 copy-start.1
  7.2 0.0 all-gather.2.cloned.1.call-start
  7.2 0.7 all-gather.2.cloned.1.call-update
  7.9 0.0 all-reduce.5.cloned.1.call-start
  8.9 0.1 copy-done
  8.9 2.0 fusion.13
  10.9 165.4 %all-gather.2.cloned.1.call-done = bf16[2560,3584]{0,1:T(8,128)(2,1)} async-done(((bf16[2560,448]{0,1:T(8,128)(2,1)}), bf16[2560,3584]{0,1:T(8,128)(2,1)}) %all-gather.2.cloned.1.call-update) | async-done | bytes 18350096 | tf_op jit(solution)/shard_map/all_gather | solution.py:10
  176.4 0.0 copy-done.1
  176.4 14.4 %convolution_convert_fusion.1 = bf16[384,3584]{1,0:T(8,128)(2,1)} fusion(bf16[2560,3584]{0,1:T(8,128)(2,1)} %all-gather.2.cloned.1.call-done, bf16[384,64]{0,1:T(8,128)(2,1)S(1)} %fusion.13, f32[1,64,2560]{2,1,0:T(8,128)S(1)} %copy-done.1, bf16[1,384,2560]{2,1,0:T(8,128)(2,1)} %param.9, pred[384]{0:T(512)(128)(4,1)S(1)} %iota_compare_fusion), kind=kOutput, calls=%fused_computation.5 | convolution fusion | flops 7183466496 | bytes 23773568 | tf_op jit(solution)/shard_map/dot_general | solution.py:29
  190.8 0.0 all-reduce.5.cloned.1.call-update
  190.8 0.0 all-reduce.7.cloned.1.call-start
  191.5 78.1 %all-reduce.5.cloned.1.call-done = bf16[384,3584]{1,0:T(8,128)(2,1)} async-done(((bf16[384,3584]{1,0:T(8,128)(2,1)}), bf16[384,3584]{1,0:T(8,128)(2,1)}) %all-reduce.5.cloned.1.call-update) | async-done | bytes 2752528 | tf_op jit(solution)/shard_map/psum | solution.py:30
  269.5 14.3 %fusion.17 = (f32[]{:T(128)}, f32[]{:T(128)}, f32[64,2560]{1,0:T(8,128)}) fusion(f32[1,64,2560]{2,1,0:T(8,128)S(1)} %copy-done.1, f32[]{:T(128)} %bitcast.71, f32[]{:T(128)S(6)} %convert_element_type.54, bf16[384,64]{0,1:T(8,128)(2,1)S(1)} %fusion.13, bf16[384,3584]{1,0:T(8,128)(2,1)} %all-reduce.5.cloned.1.call-done, ...), kind=kOutput, calls=%fused_computation.32 | convolution fusion | flops 7183237120 | bytes 24428944 | tf_op jit(solution)/shard_map/dot_general | solution.py:32
  283.9 9.7 %all-reduce.1 = (f32[]{:T(128)}, f32[]{:T(128)}) all-reduce(f32[]{:T(128)} %get-tuple-element.5, f32[]{:T(128)} %get-tuple-element.4), channel_id=1, replica_groups=mesh['task'=8,'tp'=4] {'tp'}, use_global_device_ids=true, to_apply=%region_1.2 | all-reduce | flops 2 | bytes 16 | tf_op jit(solution)/shard_map/psum | solution.py:38
  294.9 2.0 bitcast_subtract_fusion
  296.9 14.6 %convolution_convert_fusion = bf16[384,3584]{1,0:T(8,128)(2,1)} fusion(bf16[2560,3584]{0,1:T(8,128)(2,1)} %all-gather.2.cloned.1.call-done, bf16[384,64]{0,1:T(8,128)(2,1)S(1)} %fusion.13, f32[64,2560]{1,0:T(8,128)} %bitcast_subtract_fusion, bf16[1,384,2560]{2,1,0:T(8,128)(2,1)} %param.9, pred[384]{0:T(512)(128)(4,1)S(1)} %iota_compare_fusion), kind=kOutput, calls=%fused_computation.4 | convolution fusion | flops 7183630336 | bytes 23773568 | tf_op jit(solution)/shard_map/dot_general | solution.py:29
  311.5 0.0 all-reduce.7.cloned.1.call-update
  311.5 80.5 %all-reduce.7.cloned.1.call-done = bf16[384,3584]{1,0:T(8,128)(2,1)} async-done(((bf16[384,3584]{1,0:T(8,128)(2,1)}), bf16[384,3584]{1,0:T(8,128)(2,1)}) %all-reduce.7.cloned.1.call-update) | async-done | bytes 2752528 | tf_op jit(solution)/shard_map/psum | solution.py:30
  392.1 14.7 %multiply_reduce_fusion = (f32[]{:T(128)}, f32[]{:T(128)}, f32[64,2560]{1,0:T(8,128)}) fusion(f32[64,2560]{1,0:T(8,128)} %bitcast_subtract_fusion, f32[]{:T(128)} %bitcast.72, f32[]{:T(128)S(6)} %convert_element_type.54, bf16[384,64]{0,1:T(8,128)(2,1)S(1)} %fusion.13, bf16[384,3584]{1,0:T(8,128)(2,1)} %all-reduce.7.cloned.1.call-done, ...), kind=kOutput, calls=%fused_computation.38 | convolution fusion | flops 7183237120 | bytes 24428944 | tf_op jit(solution)/shard_map/dot_general | solution.py:32
  406.8 9.5 %all-reduce = (f32[]{:T(128)}, f32[]{:T(128)}) all-reduce(f32[]{:T(128)} %get-tuple-element.3, f32[]{:T(128)} %get-tuple-element.2), channel_id=1, replica_groups=mesh['task'=8,'tp'=4] {'tp'}, use_global_device_ids=true, to_apply=%region_6.7 | all-reduce | flops 2 | bytes 16 | tf_op jit(solution)/shard_map/psum | solution.py:38
  420.5 2.7 subtract_bitcast_fusion
  (1 shorter events, 0.0 us)
Async XLA Ops:
  7.2 1.8 copy-start
  7.2 169.2 %copy-start.1 = (f32[1,64,2560]{2,1,0:T(8,128)S(1)}, f32[1,64,2560]{2,1,0:T(8,128)}, u32[]{:S(2)}) copy-start(f32[1,64,2560]{2,1,0:T(8,128)} %param.13) | copy-start | bytes 1966084
  7.2 169.2 %all-gather.2.cloned.1.call-start = ((), (), s32[]{:S(2)}) async-start(), calls=%async_computation | async-start | bytes 20643840 | tf_op jit(solution)/shard_map/all_gather | solution.py:10
  7.9 261.6 %all-reduce.5.cloned.1.call-start = ((), (), s32[]{:S(2)}) async-start(), calls=%async_computation.1 | async-start | bytes 5505024 | tf_op jit(solution)/shard_map/psum | solution.py:30
  190.8 201.3 %all-reduce.7.cloned.1.call-start = ((), (), s32[]{:S(2)}) async-start(), calls=%async_computation.2 | async-start | bytes 5505024 | tf_op jit(solution)/shard_map/psum | solution.py:30
Sparse Core Ops, SparseCore 0:
  9.6 166.6 all-gather.1
  190.9 78.5 all-reduce.4
  311.6 80.3 all-reduce.6
where the time goes:
time: 430 us
  waiting for transfers between devices  325 us (76%)
  matrix products  60 us (14%)
  between operations  20.8 us (5%)
  blocking collectives  19.3 us (4%)
  other arithmetic  4.75 us (1%)
    all_gather x1, waiting for transfers between devices, shards(): down_full = lax.all_gather(down_w, 'task', axis=1, tiled=True)  165 us
    psum x2, waiting for transfers between devices, apply(): mixed = lax.psum(partial_sum.astype(jnp.bfloat16), 'tp')  159 us
    dot_general x2, matrix products, apply(): lax.dot_general(features, second, (((0,), (0,)), ((), ())), preferred_ele...  29 us
    dot_general x2, matrix products, apply(): partial_sum = jnp.dot(active, down_full, preferred_element_type=jnp.float32)  29 us
    psum x2, blocking collectives, paired_sums(): return lax.psum((jnp.sum(vector * vector), jnp.sum(vector * image)), 'tp')  19.3 us
  transfers between devices with their start and end apart: 3, of which 3 were waited for; matrix products, arithmetic and copies ran while one was open for 0% of the time, Pallas kernels for 0%

commit v1 on v0

--- a/solution.py
+++ b/solution.py
@@ -1,6 +1,10 @@
+import functools
+
 import jax
 import jax.numpy as jnp
 from jax import lax
+from jax.experimental import pallas as pl
+from jax.experimental.pallas import tpu as pltpu
 from jax.sharding import PartitionSpec as P
 
 ITERS = 2
@@ -58,6 +62,346 @@
     return (solution[None], residual[None])
 
 
+MESH = pl.DeviceIdType.MESH
+
+
+def kernel(
+    n_task, n_tp,
+    support_hbm, adapter_hbm, gate_hbm, scal_ref, w_hbm, grad_hbm,
+    sol_ref, res_ref,
+    support, adapter, grad, weights, gated, active, total, features, image0, image1,
+    part1, got1, mixed1, part2, got2, mixed2, sums, sums_got,
+    load_sem, w_send, d2d_send, w_recv, rs_send1, rs_recv1, ag_send1, ag_recv1,
+    rs_send2, rs_recv2, ag_send2, ag_recv2, sum_send, sum_recv,
+):
+    t_me, j_me = lax.axis_index("task"), lax.axis_index("tp")
+    planes = n_task // 2
+    z, core = t_me // 2, t_me % 2
+    other = 1 - core
+    blk = w_hbm.shape[0]
+    hidden = w_hbm.shape[1]
+    rows = part1.shape[2]
+    tile = next(size for size in (512, 256, 128) if hidden % size == 0)
+    n_chunk, chunk = part2.shape[0], part2.shape[3]
+
+    def block(t):
+        return weights.at[pl.ds(pl.multiple_of(t * blk, 16), blk)]
+
+    own = pltpu.make_async_copy(w_hbm, block(t_me), load_sem.at[0])
+    own.start()
+    loads = [
+        pltpu.make_async_copy(source, target, load_sem.at[1 + place])
+        for place, (source, target) in enumerate(
+            ((gate_hbm, active), (support_hbm, support), (adapter_hbm, adapter), (grad_hbm, grad))
+        )
+    ]
+    for load in loads:
+        load.start()
+
+    up, down = {"task": t_me + 2, "tp": j_me}, {"task": t_me - 2, "tp": j_me}
+    partner = {"task": 2 * z + other, "tp": j_me}
+    peers = [{"task": t_me, "tp": lax.rem(j_me + d, n_tp)} for d in range(1, n_tp)]
+
+    barrier = pltpu.get_barrier_semaphore()
+    for peer in [partner] + peers:
+        pl.semaphore_signal(barrier, inc=1, device_id=peer, device_id_type=MESH)
+
+    @pl.when(z < planes - 1)
+    def _():
+        pl.semaphore_signal(barrier, inc=1, device_id=up, device_id_type=MESH)
+
+    @pl.when(z > 0)
+    def _():
+        pl.semaphore_signal(barrier, inc=1, device_id=down, device_id_type=MESH)
+
+    pl.semaphore_wait(barrier, n_tp + lax.min(z, 1) + lax.min(planes - 1 - z, 1))
+    own.wait()
+
+    def send_block(t, target, send_sem):
+        return pltpu.make_async_remote_copy(
+            src_ref=block(t), dst_ref=block(t), send_sem=send_sem, recv_sem=w_recv.at[t],
+            device_id=target, device_id_type=MESH,
+        )
+
+    def arrived(t):
+        pltpu.make_async_copy(block(t), block(t), w_recv.at[t]).wait()
+
+    def pass_on(plane, d, from_left):
+        t = 2 * plane + core
+
+        @pl.when(d > 0)
+        def _():
+            arrived(t)
+
+        if from_left:
+            @pl.when(z < planes - 1)
+            def _():
+                send_block(t, up, w_send.at[0, t]).start()
+
+        @pl.when((z > 0) & ((d == 0) | (not from_left)))
+        def _():
+            send_block(t, down, w_send.at[1, t]).start()
+
+        send_block(t, partner, d2d_send.at[t]).start()
+
+    pass_on(z, 0, True)
+
+    loads[1].wait()
+    loads[2].wait()
+    features[...] = jnp.dot(
+        support[...], adapter[...], preferred_element_type=jnp.float32
+    ).astype(jnp.bfloat16)
+    loads[0].wait()
+    live, rate = scal_ref[0:1, 0:1], scal_ref[1:2, 0:1]
+    tokens = active.shape[0]
+    positions = lax.broadcasted_iota(jnp.int32, (tokens, tile), 0).astype(jnp.float32)
+
+    def columns(i):
+        return pl.ds(pl.multiple_of(i * tile, tile), tile)
+
+    @pl.loop(0, hidden // tile)
+    def _(i):
+        pre = active[:, columns(i)].astype(jnp.float32)
+        gated[:, columns(i)] = jnp.where(
+            positions < live, pre / (1.0 + jnp.exp(-pre)), 0.0
+        ).astype(jnp.bfloat16)
+
+    loads[3].wait()
+
+    def make_active(vector):
+        @pl.loop(0, hidden // tile)
+        def _(i):
+            inner = jnp.dot(
+                features[...], vector[:, columns(i)].astype(jnp.bfloat16),
+                preferred_element_type=jnp.float32,
+            )
+            active[:, columns(i)] = (gated[:, columns(i)].astype(jnp.float32) * inner).astype(
+                jnp.bfloat16
+            )
+            total[:, columns(i)] = jnp.zeros_like(inner)
+
+    def product(which, first, size, part, got, send_sem, recv_sem):
+        span = pl.ds(pl.multiple_of(first, 16), size)
+        partial_sum = lax.dot_general(
+            active[...], weights[span, :], (((1,), (1,)), ((), ())),
+            preferred_element_type=jnp.float32,
+        )
+        part[which] = partial_sum.astype(jnp.bfloat16).reshape(n_tp, rows, size)
+        for d in range(1, n_tp):
+            pltpu.make_async_remote_copy(
+                src_ref=part.at[which, lax.rem(j_me + d, n_tp)], dst_ref=got.at[which, d - 1],
+                send_sem=send_sem.at[which], recv_sem=recv_sem.at[which],
+                device_id=peers[d - 1], device_id_type=MESH,
+            ).start()
+
+    def reduce(which, part, got, mixed, recv_sem, send_sem, out_sem):
+        pltpu.make_async_copy(got.at[which], got.at[which], recv_sem.at[which]).wait()
+        added = part[which, j_me].astype(jnp.float32)
+        for d in range(1, n_tp):
+            added = added + got[which, d - 1].astype(jnp.float32)
+        mixed[which, j_me] = added.astype(jnp.bfloat16)
+        for d in range(1, n_tp):
+            pltpu.make_async_remote_copy(
+                src_ref=mixed.at[which, j_me], dst_ref=mixed.at[which, j_me],
+                send_sem=send_sem.at[which], recv_sem=out_sem.at[which],
+                device_id=peers[d - 1], device_id_type=MESH,
+            ).start()
+
+    def back(which, first, size, mixed, out_sem):
+        pieces = mixed.at[which, pl.ds(0, n_tp - 1)]
+        pltpu.make_async_copy(pieces, pieces, out_sem.at[which]).wait()
+        span = pl.ds(pl.multiple_of(first, 16), size)
+        whole = mixed[which].reshape(n_tp * rows, size)
+
+        @pl.loop(0, hidden // tile)
+        def _(i):
+            total[:, columns(i)] += jnp.dot(
+                whole, weights[span, columns(i)], preferred_element_type=jnp.float32
+            )
+
+    def make_image(vector, image, slot):
+        def body(i, carry):
+            second = (gated[:, columns(i)].astype(jnp.float32) * total[:, columns(i)]).astype(
+                jnp.bfloat16
+            )
+            outer = lax.dot_general(
+                features[...], second, (((0,), (0,)), ((), ())),
+                preferred_element_type=jnp.float32,
+            )
+            v = vector[:, columns(i)]
+            value = outer / live + rate * v
+            image[:, columns(i)] = value
+            return carry[0] + v * v, carry[1] + v * value
+
+        zero = jnp.zeros((vector.shape[0], tile), jnp.float32)
+        squares, crosses = lax.fori_loop(0, hidden // tile, body, (zero, zero))
+        sums[slot, 0] = jnp.broadcast_to(jnp.sum(squares, keepdims=True), (8, 128))
+        sums[slot, 1] = jnp.broadcast_to(jnp.sum(crosses, keepdims=True), (8, 128))
+        for d in range(1, n_tp):
+            pltpu.make_async_remote_copy(
+                src_ref=sums.at[slot], dst_ref=sums_got.at[slot, d - 1],
+                send_sem=sum_send.at[slot], recv_sem=sum_recv.at[slot],
+                device_id=peers[d - 1], device_id_type=MESH,
+            ).start()
+        got = sums_got.at[slot]
+        pltpu.make_async_copy(got, got, sum_recv.at[slot]).wait()
+        norm, cross = sums[slot, 0, 0:1, 0:1], sums[slot, 1, 0:1, 0:1]
+        for d in range(1, n_tp):
+            norm = norm + sums_got[slot, d - 1, 0, 0:1, 0:1]
+            cross = cross + sums_got[slot, d - 1, 1, 0:1, 0:1]
+        return norm, cross
+
+    make_active(grad)
+
+    @pl.loop(0, planes)
+    def _(d):
+        left, right = z - d, z + d
+
+        @pl.when((d > 0) & (left >= 0))
+        def _():
+            pass_on(left, d, True)
+
+        @pl.when((d > 0) & (right < planes))
+        def _():
+            pass_on(right, d, False)
+
+        for stage in range(3):
+            for plane, there in ((left, left >= 0), (right, (d > 0) & (right < planes))):
+                for side in (core, other):
+                    @pl.when(there)
+                    def _(plane=plane, side=side, mine=side is core, stage=stage):
+                        t = 2 * plane + side
+                        if stage == 0:
+                            if not mine:
+                                arrived(t)
+                            product(t, t * blk, blk, part1, got1, rs_send1, rs_recv1)
+                        elif stage == 1:
+                            reduce(t, part1, got1, mixed1, rs_recv1, ag_send1, ag_recv1)
+                        else:
+                            back(t, t * blk, blk, mixed1, ag_recv1)
+
+    norm0, cross0 = make_image(grad, image0, 0)
+    alpha0 = norm0 / cross0
+
+    @pl.loop(0, hidden // tile)
+    def _(i):
+        res_ref[:, columns(i)] = grad[:, columns(i)] - alpha0 * image0[:, columns(i)]
+
+    make_active(res_ref)
+
+    @pl.loop(0, n_chunk)
+    def _(k):
+        product(k, k * chunk, chunk, part2, got2, rs_send2, rs_recv2)
+
+    @pl.loop(0, n_chunk)
+    def _(k):
+        reduce(k, part2, got2, mixed2, rs_recv2, ag_send2, ag_recv2)
+
+    @pl.loop(0, n_chunk)
+    def _(k):
+        back(k, k * chunk, chunk, mixed2, ag_recv2)
+
+    norm1, cross1 = make_image(res_ref, image1, 1)
+    ratio = norm1 / norm0
+    alpha1 = norm1 / (cross1 - ratio * norm1 / alpha0)
+
+    @pl.loop(0, hidden // tile)
+    def _(i):
+        first, then = grad[:, columns(i)], res_ref[:, columns(i)]
+        sol_ref[:, columns(i)] = alpha0 * first + alpha1 * (then + ratio * first)
+        res_ref[:, columns(i)] = then - alpha1 * (
+            image1[:, columns(i)] + ratio * image0[:, columns(i)]
+        )
+
+    def drained(ref, sem):
+        pltpu.make_async_copy(ref, ref, sem).wait()
+
+    @pl.loop(0, n_task)
+    def _(t):
+        @pl.when((t % 2 == core) & (t // 2 <= z) & (z < planes - 1))
+        def _():
+            drained(block(t), w_send.at[0, t])
+
+        @pl.when((t % 2 == core) & (t // 2 >= z) & (z > 0))
+        def _():
+            drained(block(t), w_send.at[1, t])
+
+        @pl.when(t % 2 == core)
+        def _():
+            drained(block(t), d2d_send.at[t])
+
+        drained(got1.at[t], rs_send1.at[t])
+        drained(got1.at[t], ag_send1.at[t])
+
+    @pl.loop(0, n_chunk)
+    def _(k):
+        drained(got2.at[k], rs_send2.at[k])
+        drained(got2.at[k], ag_send2.at[k])
+
+    for slot in range(2):
+        drained(sums_got.at[slot], sum_send.at[slot])
+
+
+def fused(n_task, n_tp, support_x, adapter_a, gate_pre, lengths, damping, down_w, grad_b):
+    tokens, width = support_x.shape[1:]
+    rank = adapter_a.shape[2]
+    hidden, blk = down_w.shape
+    rows = tokens // n_tp
+    chunk = next(size for size in (512, 256, 128) if width % size == 0)
+    n_chunk = width // chunk
+    scal = jnp.broadcast_to(
+        jnp.concatenate([lengths.astype(jnp.float32), damping])[:, None], (2, 128)
+    )
+    f32, bf16 = jnp.float32, jnp.bfloat16
+    dma = pltpu.SemaphoreType.DMA
+    anywhere, vmem = pl.BlockSpec(memory_space=pl.ANY), pl.BlockSpec(memory_space=pltpu.VMEM)
+    shape = jax.ShapeDtypeStruct((rank, hidden), f32)
+    solved, residual = pl.pallas_call(
+        functools.partial(kernel, n_task, n_tp),
+        out_shape=(shape, shape),
+        in_specs=[anywhere, anywhere, anywhere, vmem, anywhere, anywhere],
+        out_specs=(vmem, vmem),
+        scratch_shapes=[
+            pltpu.VMEM((tokens, width), bf16),
+            pltpu.VMEM((width, rank), bf16),
+            pltpu.VMEM((rank, hidden), f32),
+            pltpu.VMEM((width, hidden), bf16),
+            pltpu.VMEM((tokens, hidden), bf16),
+            pltpu.VMEM((tokens, hidden), bf16),
+            pltpu.VMEM((tokens, hidden), f32),
+            pltpu.VMEM((tokens, rank), bf16),
+            pltpu.VMEM((rank, hidden), f32),
+            pltpu.VMEM((rank, hidden), f32),
+            pltpu.VMEM((n_task, n_tp, rows, blk), bf16),
+            pltpu.VMEM((n_task, n_tp - 1, rows, blk), bf16),
+            pltpu.VMEM((n_task, n_tp, rows, blk), bf16),
+            pltpu.VMEM((n_chunk, n_tp, rows, chunk), bf16),
+            pltpu.VMEM((n_chunk, n_tp - 1, rows, chunk), bf16),
+            pltpu.VMEM((n_chunk, n_tp, rows, chunk), bf16),
+            pltpu.VMEM((2, 2, 8, 128), f32),
+            pltpu.VMEM((2, n_tp - 1, 2, 8, 128), f32),
+            dma((5,)),
+            dma((2, n_task)),
+            dma((n_task,)),
+            dma((n_task,)),
+            dma((n_task,)),
+            dma((n_task,)),
+            dma((n_task,)),
+            dma((n_task,)),
+            dma((n_chunk,)),
+            dma((n_chunk,)),
+            dma((n_chunk,)),
+            dma((n_chunk,)),
+            dma((2,)),
+            dma((2,)),
+        ],
+        compiler_params=pltpu.CompilerParams(
+            collective_id=0, has_side_effects=True, vmem_limit_bytes=66_000_000
+        ),
+    )(support_x[0], adapter_a[0], gate_pre[0], scal, down_w.T, grad_b[0])
+    return solved[None], residual[None]
+
+
 def solution(mesh):
     in_specs = (
         P("task", None, None),
@@ -69,4 +413,11 @@
         P("task", None, "tp"),
     )
     out_specs = (P("task", None, "tp"), P("task", None, "tp"))
-    return jax.shard_map(shards, mesh=mesh, in_specs=in_specs, out_specs=out_specs, check_vma=False)
+    n_task, n_tp = mesh.shape["task"], mesh.shape["tp"]
+
+    def body(support_x, *rest):
+        if support_x.shape[1] % (16 * n_tp):
+            return shards(support_x, *rest)
+        return fused(n_task, n_tp, support_x, *rest)
+
+    return jax.shard_map(body, mesh=mesh, in_specs=in_specs, out_specs=out_specs, check_vma=False)

time: 430 us -> 264 us (0.61)
  waiting for transfers between devices: 325 us -> 0 us
  Pallas kernels: 0 us -> 254 us
  matrix products: 60 us -> 0 us
  blocking collectives: 19.3 us -> 0 us
  between operations: 20.8 us -> 1.93 us
  local copies, waits for them, and re-layouts: 0.1 us -> 6.84 us
  other arithmetic: 4.75 us -> 0.08 us
    pallas_call x0 -> x1, Pallas kernels: none -> 254 us  [fused(): pl.pallas_call(functools.partial(kernel, n_task, n_tp), out_shape=(shape,...]
    all_gather x1 -> x0, waiting for transfers between devices: 165 us -> none  [shards(): down_full = lax.all_gather(down_w, 'task', axis=1, tiled=True)]
    psum x2 -> x0, waiting for transfers between devices: 159 us -> none  [apply(): mixed = lax.psum(partial_sum.astype(jnp.bfloat16), 'tp')]
    dot_general x5 -> x0, matrix products: 60 us -> none  [the longest x2 29 us: apply(): lax.dot_general(features, second, (((0,), (0,)), ((), ())), preferred_ele...]
    psum x2 -> x0, blocking collectives: 19.3 us -> none  [paired_sums(): return lax.psum((jnp.sum(vector * vector), jnp.sum(vector * image)), 'tp')]
    unnamed x4 -> x3, local copies, waits for them, and re-layouts: 0.1 us -> 6.2 us
  transfers between devices with their start and end apart: 3 -> 0, of which waited for: 3 -> 0; matrix products, arithmetic and copies ran while one was open for 0% -> 0% of each run, Pallas kernels for 0% -> 0%
where the time goes in v1:
time: 264 us; the launch traced here: 263 us
  Pallas kernels  254 us (96%)
  local copies, waits for them, and re-layouts  6.84 us (3%)
    pallas_call x1, Pallas kernels, fused(): pl.pallas_call(functools.partial(kernel, n_task, n_tp), out_shape=(shape,...  254 us
    unnamed x3, local copies, waits for them, and re-layouts  6.2 us

profile of v1, /device:TPU:0, one launch (start us, length us, event | category | flops | bytes accessed | tf_op | source)
XLA Modules:
  0.0 263.3 jit_solution(15801691303166491314)
XLA Ops:
  1.9 0.1 pad_maximum_fusion
  2.0 0.6 broadcast_in_dim.12.scal_ref
  2.6 2.3 copy.9
  4.9 254.4 %shard_map.86 = (f32[64,2560]{1,0:T(8,128)}, f32[64,2560]{1,0:T(8,128)}) custom-call(bf16[384,3584]{1,0:T(8,128)(2,1)} %bitcast.8, bf16[3584,64]{1,0:T(8,128)(2,1)} %bitcast.7, bf16[384,2560]{1,0:T(8,128)(2,1)} %bitcast.10, f32[2,128]{1,0:T(2,128)} %broadcast_in_dim.12.scal_ref, bf16[448,2560]{1,0:T(8,128)(2,1)} %bitcast.9, f32[64,2560]{1,0:T(8,128)} %bitcast.11), custom_call_target="tpu_custom_call" | custom-call | tf_op jit(solution)/shard_map/pallas_call | solution.py:359
  259.3 2.0 copy.14
  261.3 2.0 copy.15

commit v2 on v1

--- a/solution.py
+++ b/solution.py
@@ -72,22 +72,24 @@
     support, adapter, grad, weights, gated, active, total, features, image0, image1,
     part1, got1, mixed1, part2, got2, mixed2, sums, sums_got,
     load_sem, w_send, d2d_send, w_recv, rs_send1, rs_recv1, ag_send1, ag_recv1,
-    rs_send2, rs_recv2, ag_send2, ag_recv2, sum_send, sum_recv,
+    rs_send2, rs_recv2, ag_send2, ag_recv2, fw_send, fw_recv, sum_send, sum_recv,
 ):
     t_me, j_me = lax.axis_index("task"), lax.axis_index("tp")
     planes = n_task // 2
     z, core = t_me // 2, t_me % 2
     other = 1 - core
-    blk = w_hbm.shape[0]
+    blk = part1.shape[3]
+    subs = w_hbm.shape[0] // blk
     hidden = w_hbm.shape[1]
     rows = part1.shape[2]
     tile = next(size for size in (512, 256, 128) if hidden % size == 0)
     n_chunk, chunk = part2.shape[0], part2.shape[3]
 
-    def block(t):
-        return weights.at[pl.ds(pl.multiple_of(t * blk, 16), blk)]
-
-    own = pltpu.make_async_copy(w_hbm, block(t_me), load_sem.at[0])
+    def block(u):
+        return weights.at[pl.ds(pl.multiple_of(u * blk, 16), blk)]
+
+    mine_all = weights.at[pl.ds(pl.multiple_of(t_me * subs * blk, 16), subs * blk)]
+    own = pltpu.make_async_copy(w_hbm, mine_all, load_sem.at[0])
     own.start()
     loads = [
         pltpu.make_async_copy(source, target, load_sem.at[1 + place])
@@ -126,8 +128,8 @@
     def arrived(t):
         pltpu.make_async_copy(block(t), block(t), w_recv.at[t]).wait()
 
-    def pass_on(plane, d, from_left):
-        t = 2 * plane + core
+    def pass_on(plane, s, d, from_left):
+        t = (2 * plane + core) * subs + s
 
         @pl.when(d > 0)
         def _():
@@ -144,7 +146,8 @@
 
         send_block(t, partner, d2d_send.at[t]).start()
 
-    pass_on(z, 0, True)
+    for s in range(subs):
+        pass_on(z, s, 0, True)
 
     loads[1].wait()
     loads[2].wait()
@@ -194,22 +197,20 @@
                 device_id=peers[d - 1], device_id_type=MESH,
             ).start()
 
-    def reduce(which, part, got, mixed, recv_sem, send_sem, out_sem):
+    def reduce(which, part, got, mixed, recv_sem, send_sem, out_sem, targets):
         pltpu.make_async_copy(got.at[which], got.at[which], recv_sem.at[which]).wait()
         added = part[which, j_me].astype(jnp.float32)
         for d in range(1, n_tp):
             added = added + got[which, d - 1].astype(jnp.float32)
         mixed[which, j_me] = added.astype(jnp.bfloat16)
-        for d in range(1, n_tp):
+        for target in targets:
             pltpu.make_async_remote_copy(
                 src_ref=mixed.at[which, j_me], dst_ref=mixed.at[which, j_me],
                 send_sem=send_sem.at[which], recv_sem=out_sem.at[which],
-                device_id=peers[d - 1], device_id_type=MESH,
+                device_id=target, device_id_type=MESH,
             ).start()
 
-    def back(which, first, size, mixed, out_sem):
-        pieces = mixed.at[which, pl.ds(0, n_tp - 1)]
-        pltpu.make_async_copy(pieces, pieces, out_sem.at[which]).wait()
+    def back(which, first, size, mixed):
         span = pl.ds(pl.multiple_of(first, 16), size)
         whole = mixed[which].reshape(n_tp * rows, size)
 
@@ -253,32 +254,35 @@
 
     make_active(grad)
 
-    @pl.loop(0, planes)
-    def _(d):
+    @pl.loop(0, planes * subs)
+    def _(e):
+        d, s = e // subs, e % subs
         left, right = z - d, z + d
 
         @pl.when((d > 0) & (left >= 0))
         def _():
-            pass_on(left, d, True)
+            pass_on(left, s, d, True)
 
         @pl.when((d > 0) & (right < planes))
         def _():
-            pass_on(right, d, False)
+            pass_on(right, s, d, False)
 
         for stage in range(3):
             for plane, there in ((left, left >= 0), (right, (d > 0) & (right < planes))):
                 for side in (core, other):
                     @pl.when(there)
                     def _(plane=plane, side=side, mine=side is core, stage=stage):
-                        t = 2 * plane + side
+                        t = (2 * plane + side) * subs + s
                         if stage == 0:
                             if not mine:
                                 arrived(t)
                             product(t, t * blk, blk, part1, got1, rs_send1, rs_recv1)
                         elif stage == 1:
-                            reduce(t, part1, got1, mixed1, rs_recv1, ag_send1, ag_recv1)
+                            reduce(t, part1, got1, mixed1, rs_recv1, ag_send1, ag_recv1, peers)
                         else:
-                            back(t, t * blk, blk, mixed1, ag_recv1)
+                            pieces = mixed1.at[t, pl.ds(0, n_tp - 1)]
+                            pltpu.make_async_copy(pieces, pieces, ag_recv1.at[t]).wait()
+                            back(t, t * blk, blk, mixed1)
 
     norm0, cross0 = make_image(grad, image0, 0)
     alpha0 = norm0 / cross0
@@ -293,13 +297,36 @@
     def _(k):
         product(k, k * chunk, chunk, part2, got2, rs_send2, rs_recv2)
 
+    row, col = j_me // 2, j_me % 2
+    beside, below = 2 * row + 1 - col, 2 * (1 - row) + col
+    half = rows // 2
+    near = [{"task": t_me, "tp": beside}, {"task": t_me, "tp": below}]
+
     @pl.loop(0, n_chunk)
     def _(k):
-        reduce(k, part2, got2, mixed2, rs_recv2, ag_send2, ag_recv2)
+        reduce(k, part2, got2, mixed2, rs_recv2, ag_send2, ag_recv2, near)
+
+    def finish(k):
+        piece = mixed2.at[k, 0]
+        pltpu.make_async_copy(piece, piece, fw_recv.at[k]).wait()
+        back(k, k * chunk, chunk, mixed2)
 
     @pl.loop(0, n_chunk)
     def _(k):
-        back(k, k * chunk, chunk, mixed2, ag_recv2)
+        pieces = mixed2.at[k, pl.ds(0, 2)]
+        pltpu.make_async_copy(pieces, pieces, ag_recv2.at[k]).wait()
+        for source, start, target in ((beside, 0, near[1]), (below, half, near[0])):
+            piece = mixed2.at[k, source, pl.ds(start, half)]
+            pltpu.make_async_remote_copy(
+                src_ref=piece, dst_ref=piece, send_sem=fw_send.at[k], recv_sem=fw_recv.at[k],
+                device_id=target, device_id_type=MESH,
+            ).start()
+
+        @pl.when(k > 0)
+        def _():
+            finish(k - 1)
+
+    finish(n_chunk - 1)
 
     norm1, cross1 = make_image(res_ref, image1, 1)
     ratio = norm1 / norm0
@@ -316,17 +343,19 @@
     def drained(ref, sem):
         pltpu.make_async_copy(ref, ref, sem).wait()
 
-    @pl.loop(0, n_task)
+    @pl.loop(0, n_task * subs)
     def _(t):
-        @pl.when((t % 2 == core) & (t // 2 <= z) & (z < planes - 1))
+        task = t // subs
+
+        @pl.when((task % 2 == core) & (task // 2 <= z) & (z < planes - 1))
         def _():
             drained(block(t), w_send.at[0, t])
 
-        @pl.when((t % 2 == core) & (t // 2 >= z) & (z > 0))
+        @pl.when((task % 2 == core) & (task // 2 >= z) & (z > 0))
         def _():
             drained(block(t), w_send.at[1, t])
 
-        @pl.when(t % 2 == core)
+        @pl.when(task % 2 == core)
         def _():
             drained(block(t), d2d_send.at[t])
 
@@ -336,7 +365,8 @@
     @pl.loop(0, n_chunk)
     def _(k):
         drained(got2.at[k], rs_send2.at[k])
-        drained(got2.at[k], ag_send2.at[k])
+        drained(mixed2.at[k, pl.ds(0, 2)], ag_send2.at[k])
+        drained(mixed2.at[k, 0], fw_send.at[k])
 
     for slot in range(2):
         drained(sums_got.at[slot], sum_send.at[slot])
@@ -345,7 +375,9 @@
 def fused(n_task, n_tp, support_x, adapter_a, gate_pre, lengths, damping, down_w, grad_b):
     tokens, width = support_x.shape[1:]
     rank = adapter_a.shape[2]
-    hidden, blk = down_w.shape
+    hidden, share = down_w.shape
+    blk = share // 2 if share % 32 == 0 else share
+    n_block = n_task * share // blk
     rows = tokens // n_tp
     chunk = next(size for size in (512, 256, 128) if width % size == 0)
     n_chunk = width // chunk
@@ -372,22 +404,24 @@
             pltpu.VMEM((tokens, rank), bf16),
             pltpu.VMEM((rank, hidden), f32),
             pltpu.VMEM((rank, hidden), f32),
-            pltpu.VMEM((n_task, n_tp, rows, blk), bf16),
-            pltpu.VMEM((n_task, n_tp - 1, rows, blk), bf16),
-            pltpu.VMEM((n_task, n_tp, rows, blk), bf16),
+            pltpu.VMEM((n_block, n_tp, rows, blk), bf16),
+            pltpu.VMEM((n_block, n_tp - 1, rows, blk), bf16),
+            pltpu.VMEM((n_block, n_tp, rows, blk), bf16),
             pltpu.VMEM((n_chunk, n_tp, rows, chunk), bf16),
             pltpu.VMEM((n_chunk, n_tp - 1, rows, chunk), bf16),
             pltpu.VMEM((n_chunk, n_tp, rows, chunk), bf16),
             pltpu.VMEM((2, 2, 8, 128), f32),
             pltpu.VMEM((2, n_tp - 1, 2, 8, 128), f32),
             dma((5,)),
-            dma((2, n_task)),
-            dma((n_task,)),
-            dma((n_task,)),
-            dma((n_task,)),
-            dma((n_task,)),
-            dma((n_task,)),
-            dma((n_task,)),
+            dma((2, n_block)),
+            dma((n_block,)),
+            dma((n_block,)),
+            dma((n_block,)),
+            dma((n_block,)),
+            dma((n_block,)),
+            dma((n_block,)),
+            dma((n_chunk,)),
+            dma((n_chunk,)),
             dma((n_chunk,)),
             dma((n_chunk,)),
             dma((n_chunk,)),
@@ -416,7 +450,7 @@
     n_task, n_tp = mesh.shape["task"], mesh.shape["tp"]
 
     def body(support_x, *rest):
-        if support_x.shape[1] % (16 * n_tp):
+        if n_tp != 4 or support_x.shape[1] % (32 * n_tp):
             return shards(support_x, *rest)
         return fused(n_task, n_tp, support_x, *rest)
 

time: 264 us -> 256 us (0.970)
  Pallas kernels: 254 us -> 247 us
    pallas_call x1, Pallas kernels: 254 us -> 247 us  [fused(): pl.pallas_call(functools.partial(kernel, n_task, n_tp), out_shape=(shape,...]
where the time goes in v2:
time: 256 us
  Pallas kernels  247 us (96%)
  local copies, waits for them, and re-layouts  6.84 us (3%)
    pallas_call x1, Pallas kernels, fused(): pl.pallas_call(functools.partial(kernel, n_task, n_tp), out_shape=(shape,...  247 us
    unnamed x3, local copies, waits for them, and re-layouts  6.2 us

profile of v2, /device:TPU:0, one launch (start us, length us, event | category | flops | bytes accessed | tf_op | source)
XLA Modules:
  0.0 255.7 jit_solution(10908779178216266176)
XLA Ops:
  1.9 0.1 pad_maximum_fusion
  2.0 0.6 broadcast_in_dim.12.scal_ref
  2.6 2.3 copy.9
  4.9 246.8 %shard_map.86 = (f32[64,2560]{1,0:T(8,128)}, f32[64,2560]{1,0:T(8,128)}) custom-call(bf16[384,3584]{1,0:T(8,128)(2,1)} %bitcast.8, bf16[3584,64]{1,0:T(8,128)(2,1)} %bitcast.7, bf16[384,2560]{1,0:T(8,128)(2,1)} %bitcast.10, f32[2,128]{1,0:T(2,128)} %broadcast_in_dim.12.scal_ref, bf16[448,2560]{1,0:T(8,128)(2,1)} %bitcast.9, f32[64,2560]{1,0:T(8,128)} %bitcast.11), custom_call_target="tpu_custom_call" | custom-call | tf_op jit(solution)/shard_map/pallas_call | solution.py:391
  251.7 2.0 copy.14
  253.7 2.0 copy.15
